TPU v7x, 256 devices: a whole 4x4x8 slice. The times are simulated.
256 devices in a mesh: row: 16 (over x_lo, y, core), col: 16 (over z, x_hi).
Axes of the slice: x: 4 (x_hi: 2, x_lo: 2; x = x_hi * 2 + x_lo), y: 4, z: 8, core: 2. Of those that a mesh axis runs over, the one named last changes fastest.
Arguments:
- orbital_factors: bfloat16 [2048, 8, 6144], P(('row', 'col')), may hold values from -0.045166016 to 0.045166016
- occ_energy: bfloat16 [8], replicated, may hold values from -2 to -0.29882812
- virt_energy: bfloat16 [2048], P(('row', 'col')), may hold values from 0.19921875 to 4
Outputs:
- pair_energy: float32 [8, 8], replicated
- virt_share: float32 [2048], P(('row', 'col'))
All inputs are finite; a program needn't handle non-finite values.
Results may differ from a plain program's by a relative error of at most 0.0003.
Values may be sent and summed in bfloat16 or wider, within the bound.
A program may use at most 64 MiB of HBM per device.

v0:
```python
import jax
import jax.numpy as jnp
from jax import lax
from jax.sharding import Mesh
from jax.sharding import PartitionSpec as P

COL = ("col_0", "col_1")
ROW = ("row_0", "row_1", "row_2")
ROW_COL = ("row_0", "row_1", "row_2", "col_0", "col_1")


def sum_by_axis(array, axes, dim):
    for axis in axes:
        array = lax.psum_scatter(array, axis, scatter_dimension=dim, tiled=True)
    return array


def over_axes(array, axes):
    for axis in axes:
        array = lax.psum(array, axis)
    return array


def occupied_major(factors):
    return jnp.transpose(factors, (1, 0, 2))


def tile_terms(occupied, narrow_side, narrow_eps, wide_side, wide_eps):
    norbit = narrow_side.shape[0]
    narrow_rows = narrow_side.shape[1]
    wide_rows = wide_side.shape[1]
    naux_width = narrow_side.shape[2]
    integral = lax.dot_general(
        narrow_side.reshape(norbit * narrow_rows, naux_width),
        wide_side.reshape(norbit * wide_rows, naux_width),
        (((1,), (1,)), ((), ())),
        preferred_element_type=jnp.float32,
    )
    integral = integral.reshape(norbit, narrow_rows, norbit, wide_rows)
    swapped = jnp.transpose(integral, (2, 1, 0, 3))
    denominator = (
        occupied[:, None, None, None]
        + occupied[None, None, :, None]
        - narrow_eps.astype(jnp.float32)[None, :, None, None]
        - wide_eps.astype(jnp.float32)[None, None, None, :]
    )
    return integral * (2.0 * integral - swapped) / denominator


def on_device(orbital_factors, occ_energy, virt_energy):
    occupied = occ_energy.astype(jnp.float32)
    gathered, gathered_eps = (
        lax.all_gather(orbital_factors, COL, axis=0, tiled=True),
        lax.all_gather(virt_energy, COL, axis=0, tiled=True),
    )
    wide_side = occupied_major(gathered)
    energy_terms = tile_terms(
        occupied,
        occupied_major(lax.all_gather(orbital_factors, ROW, axis=0, tiled=True)),
        lax.all_gather(virt_energy, ROW, axis=0, tiled=True),
        wide_side,
        gathered_eps,
    )
    pair_part = jnp.sum(energy_terms, axis=(1, 3))
    virt_part = jnp.sum(energy_terms, axis=(0, 1, 2))
    virt_share = sum_by_axis(virt_part, COL, 0)
    pair_energy = over_axes(jnp.transpose(pair_part), ROW_COL)
    return (pair_energy, virt_share)


def solution(mesh):
    split = Mesh(mesh.devices.reshape(2, 4, 2, 8, 2), ("row_0", "row_1", "row_2", "col_0", "col_1"))
    return jax.shard_map(
        on_device,
        mesh=split,
        in_specs=(P(ROW_COL, None, None), P(), P(ROW_COL)),
        out_specs=(P(), P(ROW_COL)),
        check_vma=False,
    )
```

profile of v0, /device:TPU:1, one launch (start us, length us, event | category | flops | bytes accessed | tf_op | source)
XLA Modules:
  0.0 333.8 jit_solution(7506974456959254850)
XLA Ops:
  7.2 0.0 all-gather.3.cloned.1.call-start
  7.2 2.5 copy.8
  9.7 0.0 all-gather.3.cloned.1.call-update
  9.7 0.0 all-gather.5.cloned.1.call-start
  9.8 0.7 all-gather.5.cloned.1.call-update
  10.5 1.3 dynamic-slice
  12.4 0.9 dynamic-update-slice
  13.3 30.5 %all-reduce = bf16[128]{0:T(256)(128)(2,1)S(1)} all-reduce(bf16[128]{0:T(256)(128)(2,1)S(1)} %dynamic-update-slice), channel_id=1, replica_groups=mesh['row_0'=2,'row_1'=4,'row_2'=2,'col_0'=8,'col_1'=2] {'row_0','row_1'..., use_global_device_ids=true, to_apply=%add | all-reduce | flops 128 | bytes 512
  43.8 0.7 convert_element_type.9
  44.5 1.3 dynamic-slice.1
  46.4 0.9 dynamic-update-slice.1
  47.3 37.0 %all-reduce.1 = bf16[128]{0:T(256)(128)(2,1)S(1)} all-reduce(bf16[128]{0:T(256)(128)(2,1)S(1)} %dynamic-update-slice.1), channel_id=1, replica_groups=mesh['row_0'=2,'row_1'=4,'row_2'=2,'col_0'=8,'col_1'=2] {'col_0','col_1'}, use_global_device_ids=true, to_apply=%add.1 | all-reduce | flops 128 | bytes 512
  84.3 1.3 dynamic-slice.2
  85.5 1.3 dynamic-slice.4
  88.1 0.1 broadcast_add_fusion
  88.2 0.1 broadcast_subtract_fusion
  88.2 1.5 all-gather.3.cloned.1.call-done
  89.8 180.7 %all-gather.5.cloned.1.call-done = bf16[128,8,6144]{2,0,1:T(8,128)(2,1)} async-done(((bf16[8,8,6144]{2,0,1:T(8,128)(2,1)}), bf16[128,8,6144]{2,0,1:T(8,128)(2,1)}) %all-gather.5.cloned.1.call-update) | async-done | bytes 12582928 | tf_op jit(solution)/shard_map/all_gather | solution.py:53
  270.5 16.9 %fusion = f32[8,128,8,128]{3,1,2,0:T(8,128)S(1)} fusion(bf16[128,8,6144]{2,0,1:T(8,128)(2,1)} %all-gather.5.cloned.1.call-done, bf16[128,8,6144]{2,0,1:T(8,128)(2,1)} %all-gather.3.cloned.1.call-done), kind=kOutput, calls=%fused_computation | convolution fusion | flops 12884901888 | bytes 29360128 | tf_op jit(solution)/shard_map/dot_general | solution.py:33
  287.4 2.1 fusion.5
  289.5 3.8 %psum.35 = f32[8,8]{0,1:T(8,128)S(1)} all-reduce(f32[8,8]{0,1:T(8,128)S(1)} %bitcast.27), channel_id=1, replica_groups=mesh['row_0'=2,'row_1'=4,'row_2'=2,'col_0'=8,'col_1'=2] {'row_0'}, use_global_device_ids=true, to_apply=%region_1.0 | all-reduce | flops 64 | bytes 512 | tf_op jit(solution)/shard_map/psum | solution.py:20
  293.3 8.6 %psum.36 = f32[8,8]{0,1:T(8,128)S(1)} all-reduce(f32[8,8]{0,1:T(8,128)S(1)} %psum.35), channel_id=1, replica_groups=mesh['row_0'=2,'row_1'=4,'row_2'=2,'col_0'=8,'col_1'=2] {'row_1'}, use_global_device_ids=true, to_apply=%region_2.0 | all-reduce | flops 64 | bytes 512 | tf_op jit(solution)/shard_map/psum | solution.py:20
  301.9 6.5 %psum.37 = f32[8,8]{0,1:T(8,128)S(1)} all-reduce(f32[8,8]{0,1:T(8,128)S(1)} %psum.36), channel_id=1, replica_groups=mesh['row_0'=2,'row_1'=4,'row_2'=2,'col_0'=8,'col_1'=2] {'row_2'}, use_global_device_ids=true, to_apply=%region_3.0 | all-reduce | flops 64 | bytes 512 | tf_op jit(solution)/shard_map/psum | solution.py:20
  308.4 12.0 %all-reduce.4 = (f32[8,8]{0,1:T(8,128)S(1)}, f32[128]{0:T(128)S(1)}) all-reduce(f32[8,8]{0,1:T(8,128)S(1)} %psum.37, f32[128]{0:T(128)S(1)} %get-tuple-element.4), channel_id=1, replica_groups=mesh['row_0'=2,'row_1'=4,'row_2'=2,'col_0'=8,'col_1'=2] {'col_0'}, use_global_device_ids=true, to_apply=%region_4.0 | all-reduce | flops 192 | bytes 1536 | tf_op jit(solution)/shard_map/psum | solution.py:20
  320.4 0.1 dynamic-slice.3
  320.4 5.3 %all-reduce.5 = (f32[8,8]{0,1:T(8,128)S(1)}, f32[16]{0:T(128)S(1)}) all-reduce(f32[8,8]{0,1:T(8,128)S(1)} %get-tuple-element.6, f32[16]{0:T(128)S(1)} %dynamic-slice.3), channel_id=1, replica_groups=mesh['row_0'=2,'row_1'=4,'row_2'=2,'col_0'=8,'col_1'=2] {'col_1'}, use_global_device_ids=true, to_apply=%region_5.0 | all-reduce | flops 80 | bytes 640 | tf_op jit(solution)/shard_map/psum | solution.py:20
  325.8 0.7 copy.11
  326.4 0.6 dynamic-slice.5
  (4 shorter events, 0.0 us)
Async XLA Ops:
  7.2 82.6 %all-gather.3.cloned.1.call-start = ((), (), s32[]{:S(2)}) async-start(), calls=%async_computation | async-start | bytes 13369344 | tf_op jit(solution)/shard_map/all_gather | solution.py:59
  9.7 260.7 %all-gather.5.cloned.1.call-start = ((), (), s32[]{:S(2)}) async-start(), calls=%async_computation.1 | async-start | bytes 13369344 | tf_op jit(solution)/shard_map/all_gather | solution.py:53
Sparse Core Ops, SparseCore 0:
  9.9 79.8 all-gather.2
  92.4 178.0 all-gather.4
where the time goes:
time: 337 us; the launch traced here: 334 us
  waiting for transfers between devices  183 us (54%)
  blocking collectives  104 us (31%)
  matrix products  16.9 us (5%)
  between operations  16.7 us (5%)
  local copies, waits for them, and re-layouts  10.6 us (3%)
    all_gather x1, waiting for transfers between devices, on_device(): lax.all_gather(orbital_factors, COL, axis=0, tiled=True)  181 us
    unnamed x2, blocking collectives  67.5 us
    psum x5, blocking collectives, over_axes(): array = lax.psum(array, axis)  36.2 us
    dot_general x1, matrix products, tile_terms(): lax.dot_general(narrow_side.reshape(norbit * narrow_rows, naux_width), wi...  16.9 us
    unnamed x12, local copies, waits for them, and re-layouts  10.6 us
  transfers between devices with their start and end apart: 2, of which 2 were waited for; matrix products, arithmetic and copies ran while one was open for 2% of the time, Pallas kernels for 0%

commit v1 on v0

v1 whole, which is shorter than its diff:
```python
import functools

import jax
import jax.numpy as jnp
import numpy as np
from jax import lax
from jax.experimental import pallas as pl
from jax.experimental.pallas import tpu as pltpu
from jax.sharding import PartitionSpec as P

OFFSETS = (
    (0, 1, 7),
    (0, 3, 7),
    (1, 3, 3),
    (2, 3, 7),
    (0, 0, 7),
    (0, 2, 7),
    (2, 2, 7),
    (1, 0, 0),
    (2, 0, 3),
    (3, 0, 2),
    (2, 0, 2),
    (1, 3, 7),
    (3, 0, 1),
    (0, 0, 1),
    (1, 0, 3),
    (0, 0, 0),
)
COLS = 8
ROW0 = 5
NROW = 11
FIRST = 0
LAST = 5
PLAN = (
    (1, 0, 15, 0, 7), (1, 0, 15, 4, 13), (1, 0, 15, 5, 4), (1, 1, 15, 0, 7), (1, 1, 15, 4, 13), (1, 1, 15, 5, 4),
    (1, 2, 15, 0, 7), (1, 2, 15, 4, 13), (1, 2, 15, 5, 4), (0, 0, 4, 0, 0), (0, 0, 7, 0, 0), (0, 0, 13, 0, 0),
    (1, 0, 4, 2, 0), (1, 0, 4, 3, 1), (1, 0, 13, 1, 12), (1, 3, 15, 0, 7), (1, 3, 15, 4, 13), (1, 3, 15, 5, 4),
    (0, 1, 4, 0, 0), (0, 1, 7, 0, 0), (0, 1, 13, 0, 0), (1, 1, 4, 2, 0), (1, 1, 4, 3, 1), (1, 1, 13, 1, 12),
    (1, 4, 15, 5, 4), (0, 0, 0, 0, 0), (0, 0, 1, 0, 0), (0, 0, 12, 0, 0), (1, 0, 0, 2, 5), (1, 0, 1, 0, 11),
    (1, 0, 12, 4, 9), (0, 2, 4, 0, 0), (0, 2, 7, 0, 0), (0, 2, 13, 0, 0), (1, 2, 4, 2, 0), (1, 2, 4, 3, 1),
    (1, 2, 13, 1, 12), (1, 5, 15, 5, 4), (0, 1, 0, 0, 0), (0, 1, 1, 0, 0), (0, 1, 12, 0, 0), (1, 1, 1, 0, 11),
    (1, 1, 12, 4, 9), (1, 1, 0, 2, 5), (0, 3, 4, 0, 0), (0, 3, 7, 0, 0), (0, 3, 13, 0, 0), (1, 3, 4, 3, 1),
    (1, 3, 13, 1, 12), (1, 4, 15, 4, 13), (0, 0, 5, 0, 0), (0, 2, 1, 0, 0), (0, 2, 12, 0, 0), (1, 3, 4, 2, 0),
    (0, 0, 9, 0, 0), (0, 0, 11, 0, 0), (0, 4, 4, 0, 0), (1, 0, 9, 1, 10), (1, 0, 11, 0, 3), (1, 4, 4, 3, 1),
    (1, 2, 1, 0, 11), (1, 2, 12, 4, 9), (0, 2, 0, 0, 0), (0, 3, 1, 0, 0), (0, 3, 12, 0, 0), (1, 2, 0, 2, 5),
    (0, 1, 9, 0, 0), (0, 1, 11, 0, 0), (0, 5, 4, 0, 0), (1, 1, 9, 1, 10), (1, 5, 4, 3, 1), (1, 1, 11, 0, 3),
    (1, 5, 15, 4, 13), (0, 0, 10, 0, 0), (0, 1, 5, 0, 0), (0, 4, 1, 0, 0), (1, 4, 4, 2, 0), (0, 0, 3, 0, 0),
    (0, 4, 13, 0, 0), (1, 0, 3, 3, 6), (1, 4, 13, 1, 12), (1, 0, 10, 4, 8), (1, 3, 1, 0, 11), (0, 1, 10, 0, 0),
    (0, 3, 0, 0, 0), (0, 5, 1, 0, 0), (1, 3, 0, 2, 5), (0, 2, 9, 0, 0), (0, 2, 11, 0, 0), (1, 2, 9, 1, 10),
    (1, 2, 11, 0, 3), (1, 3, 12, 4, 9), (0, 0, 6, 0, 0), (0, 2, 5, 0, 0), (0, 4, 12, 0, 0), (1, 5, 4, 2, 0),
    (0, 1, 3, 0, 0), (0, 5, 13, 0, 0), (1, 1, 3, 3, 6), (1, 5, 13, 1, 12), (1, 1, 10, 4, 8), (1, 4, 1, 0, 11),
    (0, 2, 10, 0, 0), (0, 4, 0, 0, 0), (1, 4, 0, 2, 5), (0, 0, 8, 0, 0), (0, 3, 11, 0, 0), (1, 0, 8, 1, 14),
    (1, 3, 11, 0, 3), (1, 4, 12, 4, 9), (0, 1, 6, 0, 0), (0, 3, 5, 0, 0), (0, 5, 12, 0, 0), (0, 2, 3, 0, 0),
    (0, 3, 9, 0, 0), (1, 2, 3, 3, 6), (1, 3, 9, 1, 10), (1, 2, 10, 4, 8), (1, 5, 1, 0, 11), (0, 0, 14, 0, 0),
    (0, 5, 0, 0, 0), (1, 0, 14, 3, 2), (1, 5, 0, 2, 5), (0, 1, 8, 0, 0), (0, 4, 11, 0, 0), (1, 1, 8, 1, 14),
    (1, 4, 11, 0, 3), (1, 5, 12, 4, 9), (0, 2, 6, 0, 0), (0, 3, 10, 0, 0), (0, 4, 5, 0, 0), (0, 3, 3, 0, 0),
    (0, 4, 9, 0, 0), (1, 3, 3, 3, 6), (1, 4, 9, 1, 10), (1, 3, 10, 4, 8), (0, 0, 2, 0, 0), (0, 1, 14, 0, 0),
    (0, 5, 5, 0, 0), (1, 1, 14, 3, 2), (0, 2, 8, 0, 0), (0, 5, 11, 0, 0), (1, 2, 8, 1, 14), (1, 5, 11, 0, 3),
    (1, 4, 15, 0, 7), (0, 3, 6, 0, 0), (0, 4, 10, 0, 0), (1, 4, 10, 4, 8), (0, 4, 3, 0, 0), (0, 5, 9, 0, 0),
    (1, 4, 3, 3, 6), (1, 5, 9, 1, 10), (1, 5, 15, 0, 7), (0, 1, 2, 0, 0), (0, 2, 14, 0, 0), (1, 2, 14, 3, 2),
    (0, 3, 8, 0, 0), (0, 5, 3, 0, 0), (1, 3, 8, 1, 14), (1, 5, 3, 3, 6), (0, 4, 6, 0, 0), (0, 5, 10, 0, 0),
    (1, 5, 10, 4, 8), (0, 4, 7, 0, 0), (0, 4, 8, 0, 0), (1, 4, 8, 1, 14), (0, 2, 2, 0, 0), (0, 3, 14, 0, 0),
    (1, 3, 14, 3, 2), (0, 5, 7, 0, 0), (0, 5, 8, 0, 0), (1, 5, 8, 1, 14), (0, 4, 14, 0, 0), (0, 5, 6, 0, 0),
    (1, 4, 14, 3, 2), (0, 3, 2, 0, 0), (0, 5, 14, 0, 0), (1, 5, 14, 3, 2), (0, 4, 2, 0, 0), (0, 5, 2, 0, 0),
)


NSLOT = len(OFFSETS)
CHUNKS = 1 + max(item[1] for item in PLAN)
OWN = OFFSETS.index((0, 0, 0))
STEPS = ((1, 0, 0), (3, 0, 0), (0, 1, 0), (0, 3, 0), (0, 0, 1), (0, 0, 7))
SIDES = (4, 4, 8)
MESH = pl.DeviceIdType.MESH
NI = 8
F32 = jnp.float32


def difference(first, second):
    return tuple((a - b) % side for a, b, side in zip(first, second, SIDES))


def weight_table():
    seen = set()
    table = np.zeros((NROW, 1, 128), np.float32)
    for row in range(NROW):
        for col in range(COLS):
            step = difference(OFFSETS[ROW0 + row], OFFSETS[col])
            back = difference((0, 0, 0), step)
            if min(step, back) in seen:
                continue
            seen.add(min(step, back))
            table[row, 0, col * 16 : col * 16 + 16] = 0.5 if step == back else 1.0
    assert len(seen) == 68
    return table


def kernel(
    x_ref, eps_ref, occ_ref, weight_ref, out_ref,
    raw, buf, acc, accr, epsbuf, epspart, pair_acc, square, vsrc, vrecv, csrc, crecv,
    plane, line,
    in_sem, part_send, part_recv, ring_send, ring_recv, eps_send, eps_recv,
    acc_send, acc_recv, v_send, v_recv, p_send, p_recv, l_send, l_recv,
):
    row = lax.axis_index("row")
    col = lax.axis_index("col")
    core = row % 2
    other = 1 - core
    cy = (row // 2) % 4
    cx = (col % 2) * 2 + row // 8
    cz = col // 2

    def device(step, which):
        x = (cx + step[0]) % 4
        y = (cy + step[1]) % 4
        z = (cz + step[2]) % 8
        return ((x % 2) * 8 + y * 2 + which, z * 2 + x // 2)

    partner = device((0, 0, 0), other)
    pending = []

    def send(src, dst, send_sem, recv_sem, target):
        copy = pltpu.make_async_remote_copy(
            src_ref=src, dst_ref=dst, send_sem=send_sem, recv_sem=recv_sem,
            device_id=target, device_id_type=MESH,
        )
        copy.start()
        pending.append(copy)
        return copy

    def arrived(ref, send_sem, recv_sem, target):
        pltpu.make_async_remote_copy(
            src_ref=ref, dst_ref=ref, send_sem=send_sem, recv_sem=recv_sem,
            device_id=target, device_id_type=MESH,
        ).wait_recv()

    half = x_ref.shape[1] // 2
    width = half // CHUNKS
    mine = pl.ds(pl.multiple_of(core * 64, 64), 64)
    theirs = pl.ds(pl.multiple_of(other * 64, 64), 64)
    local = pltpu.make_async_copy(
        x_ref.at[:, pl.ds(pl.multiple_of(core * half, 128), half)], raw.at[mine], in_sem
    )
    send(
        x_ref.at[:, pl.ds(pl.multiple_of(other * half, 128), half)], raw.at[mine],
        part_send.at[0], part_recv.at[0], partner,
    )
    local.start()
    send(eps_ref, epspart, part_send.at[1], part_recv.at[1], partner)

    lane = lax.broadcasted_iota(jnp.int32, (1, 128), 1)
    lane8 = lax.broadcasted_iota(jnp.int32, (8, 128), 1)
    sub8 = lax.broadcasted_iota(jnp.int32, (8, 128), 0)
    to = lax.broadcasted_iota(jnp.int32, (128, 128), 0)
    source = lax.broadcasted_iota(jnp.int32, (128, 128), 1)
    order = (source == ((to // 8) % 2) * 64 + (to % 8) * 8 + to // 16).astype(F32).astype(jnp.bfloat16)

    local.wait()
    arrived(raw.at[theirs], part_send.at[0], part_recv.at[0], partner)

    ready = set()

    def prepare(chunk):
        if chunk in ready:
            return
        ready.add(chunk)
        piece = raw[:, chunk * width : (chunk + 1) * width]
        buf[chunk, OWN] = jnp.dot(order, piece, preferred_element_type=F32).astype(jnp.bfloat16)

    def multiply(chunk, pair, first):
        count = min(2, NROW - 2 * pair)
        left = buf[chunk, ROW0 + 2 * pair : ROW0 + 2 * pair + count].reshape(count * 128, width)

        def one(block, carry):
            at = pl.multiple_of(block * 32, 32)
            right = jnp.concatenate(
                [
                    buf[chunk, 0:COLS, pl.ds(at + 16 * j, 16), :].reshape(COLS * 16, width)
                    for j in range(2)
                ],
                axis=0,
            )
            part = lax.dot_general(
                left, right, (((1,), (1,)), ((), ())), preferred_element_type=F32
            ).reshape(count, NI, 2, 8, 256)
            lanes = pl.ds(pl.multiple_of(block * 256, 256), 256)
            for k in range(count):
                for h in range(2):
                    where = (2 * pair + k, h, slice(None), slice(None), lanes)
                    if first:
                        acc[where] = part[k, :, h]
                    else:
                        acc[where] += part[k, :, h]
            return carry

        lax.fori_loop(0, 4, one, 0)

    def eps_exchange():
        arrived(epspart, part_send.at[1], part_recv.at[1], partner)
        epsbuf[OWN] = jnp.where((lane // 8) % 2 == core, eps_ref[...], epspart[...])
        for slot in range(NSLOT):
            if slot != OWN:
                send(
                    epsbuf.at[OWN], epsbuf.at[slot], eps_send.at[slot], eps_recv.at[slot],
                    device(OFFSETS[slot], core),
                )

    npair = (NROW + 1) // 2
    left_in = [NSLOT - 1] * CHUNKS
    queue = []
    sent = 0
    for kind, chunk, slot, step, target in PLAN:
        if kind == 0:
            arrived(
                buf.at[chunk, slot], ring_send.at[chunk, slot], ring_recv.at[chunk, slot], partner
            )
            left_in[chunk] -= 1
            if queue:
                multiply(*queue.pop(0))
            if left_in[chunk] == 0:
                queue += [(chunk, pair, chunk == FIRST) for pair in range(npair)]
        else:
            if slot == OWN:
                prepare(chunk)
            send(
                buf.at[chunk, slot], buf.at[chunk, target],
                ring_send.at[chunk, target], ring_recv.at[chunk, target],
                device(STEPS[step], core),
            )
            sent += 1
            if sent == 12:
                eps_exchange()

    def give(pair):
        for k in range(2 * pair, min(2 * pair + 2, NROW)):
            send(acc.at[k, other], accr.at[k], acc_send.at[k], acc_recv.at[k], partner)

    done = []
    while queue:
        chunk, pair, first = queue.pop(0)
        multiply(chunk, pair, first)
        if chunk == LAST:
            give(pair)
            done.append(pair)
    assert len(done) == npair

    for slot in range(NSLOT):
        if slot != OWN:
            arrived(epsbuf.at[slot], eps_send.at[slot], eps_recv.at[slot], partner)
    virt_col = jnp.zeros((1, 128), F32)
    for slot in range(COLS):
        virt_col = jnp.where(lane // 16 == slot, epsbuf[slot], virt_col)
    virt_col = jnp.broadcast_to(virt_col, (8, 128))
    pair_acc[...] = jnp.zeros_like(pair_acc)
    square[...] = jnp.zeros_like(square)

    def energy(k, col_sum):
        arrived(accr.at[k], acc_send.at[k], acc_recv.at[k], partner)
        spread = jnp.broadcast_to(epsbuf[ROW0 + k], (8, 128))
        virt_row = jnp.sum(
            jnp.where(lane8 == 8 * core + sub8, spread, 0.0), axis=1, keepdims=True
        )
        virt = virt_row + virt_col
        weight = jnp.broadcast_to(weight_ref[k], (8, 128))
        total = jnp.zeros((8, 128), F32)
        count = 0
        for i in range(NI):
            for j in range(i, NI):
                here = slice(128 * j, 128 * j + 128)
                there = slice(128 * i, 128 * i + 128)
                scale = weight / ((occ_ref[i] + occ_ref[j]) - virt)
                t = acc[k, core, i, :, here] + accr[k, i, :, here]
                if i == j:
                    term = t * t * scale
                    pair_acc[count] += 2.0 * term
                else:
                    s = acc[k, core, j, :, there] + accr[k, j, :, there]
                    term = (t * (2.0 * t - s) + s * (2.0 * s - t)) * scale
                    pair_acc[count] += term
                total += term
                count += 1
        square[pl.ds(pl.multiple_of(k * 8, 8), 8), :] = total
        return col_sum + total

    col_sum = lax.fori_loop(0, NROW, energy, jnp.zeros((8, 128), F32))
    vsrc[:, 0:128] = jnp.sum(square[...].T, axis=0, keepdims=True)
    vsrc[:, 128:256] = jnp.sum(col_sum, axis=0, keepdims=True)

    here = cx * 4 + cy
    count = 0
    square[...] = jnp.zeros_like(square)
    for i in range(NI):
        for j in range(i, NI):
            total = jnp.sum(pair_acc[count], axis=0, keepdims=True)
            square[i * 8 + j : i * 8 + j + 1, :] = total
            square[j * 8 + i : j * 8 + i + 1, :] = total
            count += 1
    plane[here] = jnp.sum(square[...].T, axis=0, keepdims=True)
    for m in range(1, 16):
        send(
            plane.at[here], plane.at[here], p_send.at[m], p_recv.at[m],
            device((m // 4, m % 4, 0), core),
        )

    used = [s for s in range(NSLOT) if s != OWN and (s < COLS or ROW0 <= s < ROW0 + NROW)]
    for slot in used:
        step = difference((0, 0, 0), OFFSETS[slot])
        send(vsrc, vrecv.at[slot], v_send.at[slot], v_recv.at[slot], device(step, core))
    row_total = jnp.zeros((1, 128), F32)
    col_total = jnp.zeros((1, 128), F32)
    for slot in used + [OWN]:
        if slot == OWN:
            message = vsrc[...]
        else:
            arrived(vrecv.at[slot], v_send.at[slot], v_recv.at[slot], partner)
            message = vrecv[slot]
        if ROW0 <= slot < ROW0 + NROW:
            row_total += jnp.where(lane // 8 == slot - ROW0, message[:, 0:128], 0.0)
        if slot < COLS:
            col_total += jnp.where(lane // 16 == slot, message[:, 128:256], 0.0)
    csrc[...] = col_total
    send(csrc, crecv, part_send.at[2], part_recv.at[2], partner)

    def gathered(ref, index, send_sem, recv_sem):
        arrived(ref.at[index], send_sem, recv_sem, partner)

    for m in range(1, 16):
        x = (cx + 4 - m // 4) % 4
        y = (cy + 4 - m % 4) % 4
        gathered(plane, x * 4 + y, p_send.at[m], p_recv.at[m])
    now = cz * 2 + core
    line[now] = jnp.sum(plane[...], axis=0)
    for m in range(1, 16):
        which = core if m % 2 == 0 else other
        send(
            line.at[now], line.at[now], l_send.at[m], l_recv.at[m],
            device((0, 0, m // 2), which),
        )
    arrived(crecv, part_send.at[2], part_recv.at[2], partner)
    virt = row_total + jnp.where((lane // 8) % 2 == core, col_total + crecv[...], 0.0)

    def fold(value):
        for shift in (64, 32, 16, 8):
            value = value + pltpu.roll(value, shift, 1)
        return value

    out_ref[8:16, :] = fold(jnp.broadcast_to(virt, (8, 128)))
    for m in range(1, 16):
        z = (cz + 8 - m // 2) % 8
        which = core if m % 2 == 0 else other
        gathered(line, z * 2 + which, l_send.at[m], l_recv.at[m])
    total = jnp.broadcast_to(jnp.sum(line[...], axis=0), (8, 128))
    out_ref[0:8, :] = fold(jnp.where(lane8 // 8 == sub8, total, 0.0))
    for copy in pending:
        copy.wait_send()


def on_device(orbital_factors, occ_energy, virt_energy):
    naux = orbital_factors.shape[2]
    width = naux // 2 // CHUNKS
    eps = jnp.tile(virt_energy.astype(F32), 16).reshape(1, 128)
    vmem = pl.BlockSpec(memory_space=pltpu.VMEM)
    dma = pltpu.SemaphoreType.DMA
    out = pl.pallas_call(
        kernel,
        out_shape=jax.ShapeDtypeStruct((16, 128), F32),
        in_specs=[pl.BlockSpec(memory_space=pl.ANY), vmem, pl.BlockSpec(memory_space=pltpu.SMEM), vmem],
        out_specs=vmem,
        scratch_shapes=[
            pltpu.VMEM((128, naux // 2), jnp.bfloat16),
            pltpu.VMEM((CHUNKS, NSLOT, 128, width), jnp.bfloat16),
            pltpu.VMEM((NROW, 2, NI, 8, 1024), F32),
            pltpu.VMEM((NROW, NI, 8, 1024), F32),
            pltpu.VMEM((NSLOT, 1, 128), F32),
            pltpu.VMEM((1, 128), F32),
            pltpu.VMEM((36, 8, 128), F32),
            pltpu.VMEM((128, 128), F32),
            pltpu.VMEM((1, 256), F32),
            pltpu.VMEM((NSLOT, 1, 256), F32),
            pltpu.VMEM((1, 128), F32),
            pltpu.VMEM((1, 128), F32),
            pltpu.VMEM((16, 1, 128), F32),
            pltpu.VMEM((16, 1, 128), F32),
            dma(()),
            dma((3,)), dma((3,)),
            dma((CHUNKS, NSLOT)), dma((CHUNKS, NSLOT)),
            dma((NSLOT,)), dma((NSLOT,)),
            dma((NROW,)), dma((NROW,)),
            dma((NSLOT,)), dma((NSLOT,)),
            dma((16,)), dma((16,)),
            dma((16,)), dma((16,)),
        ],
        compiler_params=pltpu.CompilerParams(
            has_side_effects=True, vmem_limit_bytes=60 * 2**20
        ),
    )(
        orbital_factors.reshape(-1, naux), eps, occ_energy.astype(F32), jnp.asarray(weight_table()),
    )
    return out[0:8, 0:8], out[8, 0:8]


def solution(mesh):
    return jax.shard_map(
        on_device,
        mesh=mesh,
        in_specs=(P(("row", "col"), None, None), P(), P(("row", "col"))),
        out_specs=(P(), P(("row", "col"))),
        check_vma=False,
    )
```

time: 337 us -> 132 us (0.39)
  waiting for transfers between devices: 183 us -> 0 us
  Pallas kernels: 0 us -> 127 us
  blocking collectives: 104 us -> 0 us
  matrix products: 16.9 us -> 0 us
  between operations: 16.7 us -> 0.65 us
  local copies, waits for them, and re-layouts: 10.6 us -> 3.85 us
    all_gather x2 -> x0, waiting for transfers between devices: 182 us -> none  [the longest x1 181 us: on_device(): lax.all_gather(orbital_factors, COL, axis=0, tiled=True)]
    pallas_call x0 -> x1, Pallas kernels: none -> 127 us  [on_device(): pl.pallas_call(kernel, out_shape=jax.ShapeDtypeStruct((16, 128), F32), in...]
    unnamed x2 -> x0, blocking collectives: 67.5 us -> none
    psum x5 -> x0, blocking collectives: 36.2 us -> none  [over_axes(): array = lax.psum(array, axis)]
    dot_general x1 -> x0, matrix products: 16.9 us -> none  [tile_terms(): lax.dot_general(narrow_side.reshape(norbit * narrow_rows, naux_width), wi...]
    unnamed x12 -> x4, local copies, waits for them, and re-layouts: 10.6 us -> 0.79 us
  transfers between devices with their start and end apart: 2 -> 0, of which waited for: 2 -> 0; matrix products, arithmetic and copies ran while one was open for 2% -> 0% of each run, Pallas kernels for 0% -> 0%
where the time goes in v1:
time: 132 us
  Pallas kernels  127 us (96%)
  local copies, waits for them, and re-layouts  3.85 us (3%)
    pallas_call x1, Pallas kernels, on_device(): pl.pallas_call(kernel, out_shape=jax.ShapeDtypeStruct((16, 128), F32), in...  127 us

profile of v1, /device:TPU:1, one launch (start us, length us, event | category | flops | bytes accessed | tf_op | source)
XLA Modules:
  0.0 131.8 jit_solution(11463828102537354611)
XLA Ops:
  0.6 0.0 copy-start.1
  0.6 0.6 copy-done.1
  1.3 0.0 copy-start
  1.3 0.5 convert_element_type.7.occ_ref
  1.8 0.1 copy-done
  1.9 0.6 reshape_tile.3.eps_ref
  2.5 126.8 %shard_map.59 = f32[16,128]{1,0:T(8,128)} custom-call(bf16[64,6144]{1,0:T(8,128)(2,1)} %bitcast.3, f32[1,128]{1,0:T(1,128)} %reshape_tile.3.eps_ref, f32[8]{0:T(128)} %convert_element_type.7.occ_ref, f32[11,1,128]{2,1,0:T(1,128)} %constant.2.clone.weight_ref), custom_call_target="tpu_custom_call" | custom-call | tf_op jit(solution)/shard_map/pallas_call | solution.py:363
  129.3 1.2 slice_bitcast_fusion
  130.5 1.3 slice.6
  (1 shorter events, 0.0 us)
Async XLA Ops:
  0.6 0.7 copy-start.1
  1.3 0.7 copy-start

commit v2 on v1

--- a/solution.py
+++ b/solution.py
@@ -72,6 +72,7 @@
 SIDES = (4, 4, 8)
 MESH = pl.DeviceIdType.MESH
 NI = 8
+GROUP = 4
 F32 = jnp.float32
 
 
@@ -133,6 +134,21 @@
             device_id=target, device_id_type=MESH,
         ).wait_recv()
 
+    peers = {(0, 0, 0, 1)}
+    for offset in OFFSETS:
+        peers |= {offset + (0,), difference((0, 0, 0), offset) + (0,)}
+    peers |= {step + (0,) for step in STEPS}
+    peers |= {(m // 4, m % 4, 0, 0) for m in range(16)}
+    peers |= {(0, 0, m // 2, m % 2) for m in range(16)}
+    peers -= {(0, 0, 0, 0)}
+    barrier = pltpu.get_barrier_semaphore()
+    for peer in sorted(peers):
+        pl.semaphore_signal(
+            barrier, inc=1, device_id=device(peer[:3], other if peer[3] else core),
+            device_id_type=MESH,
+        )
+    pl.semaphore_wait(barrier, len(peers))
+
     half = x_ref.shape[1] // 2
     width = half // CHUNKS
     mine = pl.ds(pl.multiple_of(core * 64, 64), 64)
@@ -166,33 +182,26 @@
         piece = raw[:, chunk * width : (chunk + 1) * width]
         buf[chunk, OWN] = jnp.dot(order, piece, preferred_element_type=F32).astype(jnp.bfloat16)
 
-    def multiply(chunk, pair, first):
-        count = min(2, NROW - 2 * pair)
-        left = buf[chunk, ROW0 + 2 * pair : ROW0 + 2 * pair + count].reshape(count * 128, width)
-
-        def one(block, carry):
-            at = pl.multiple_of(block * 32, 32)
-            right = jnp.concatenate(
-                [
-                    buf[chunk, 0:COLS, pl.ds(at + 16 * j, 16), :].reshape(COLS * 16, width)
-                    for j in range(2)
-                ],
-                axis=0,
-            )
+    def multiply(chunk, block):
+        right = jnp.concatenate(
+            [
+                buf[chunk, 0:COLS, 16 * j : 16 * j + 16, :].reshape(COLS * 16, width)
+                for j in (2 * block, 2 * block + 1)
+            ],
+            axis=0,
+        )
+        lanes = slice(256 * block, 256 * block + 256)
+        for k in range(0, NROW, GROUP):
+            count = min(GROUP, NROW - k)
+            left = buf[chunk, ROW0 + k : ROW0 + k + count].reshape(count * 128, width)
             part = lax.dot_general(
                 left, right, (((1,), (1,)), ((), ())), preferred_element_type=F32
             ).reshape(count, NI, 2, 8, 256)
-            lanes = pl.ds(pl.multiple_of(block * 256, 256), 256)
-            for k in range(count):
-                for h in range(2):
-                    where = (2 * pair + k, h, slice(None), slice(None), lanes)
-                    if first:
-                        acc[where] = part[k, :, h]
-                    else:
-                        acc[where] += part[k, :, h]
-            return carry
-
-        lax.fori_loop(0, 4, one, 0)
+            for h in range(2):
+                if chunk == FIRST:
+                    acc[k : k + count, h, :, :, lanes] = part[:, :, h]
+                else:
+                    acc[k : k + count, h, :, :, lanes] += part[:, :, h]
 
     def eps_exchange():
         arrived(epspart, part_send.at[1], part_recv.at[1], partner)
@@ -204,7 +213,6 @@
                     device(OFFSETS[slot], core),
                 )
 
-    npair = (NROW + 1) // 2
     left_in = [NSLOT - 1] * CHUNKS
     queue = []
     sent = 0
@@ -217,7 +225,7 @@
             if queue:
                 multiply(*queue.pop(0))
             if left_in[chunk] == 0:
-                queue += [(chunk, pair, chunk == FIRST) for pair in range(npair)]
+                queue += [(chunk, block) for block in range(4)]
         else:
             if slot == OWN:
                 prepare(chunk)
@@ -230,18 +238,14 @@
             if sent == 12:
                 eps_exchange()
 
-    def give(pair):
-        for k in range(2 * pair, min(2 * pair + 2, NROW)):
-            send(acc.at[k, other], accr.at[k], acc_send.at[k], acc_recv.at[k], partner)
-
-    done = []
-    while queue:
-        chunk, pair, first = queue.pop(0)
-        multiply(chunk, pair, first)
+    for chunk, block in queue:
+        multiply(chunk, block)
         if chunk == LAST:
-            give(pair)
-            done.append(pair)
-    assert len(done) == npair
+            lanes = slice(256 * block, 256 * block + 256)
+            send(
+                acc.at[:, other, :, :, lanes], accr.at[:, :, :, lanes],
+                acc_send.at[block], acc_recv.at[block], partner,
+            )
 
     for slot in range(NSLOT):
         if slot != OWN:
@@ -253,8 +257,11 @@
     pair_acc[...] = jnp.zeros_like(pair_acc)
     square[...] = jnp.zeros_like(square)
 
+    for block in range(4):
+        lanes = slice(256 * block, 256 * block + 256)
+        arrived(accr.at[:, :, :, lanes], acc_send.at[block], acc_recv.at[block], partner)
+
     def energy(k, col_sum):
-        arrived(accr.at[k], acc_send.at[k], acc_recv.at[k], partner)
         spread = jnp.broadcast_to(epsbuf[ROW0 + k], (8, 128))
         virt_row = jnp.sum(
             jnp.where(lane8 == 8 * core + sub8, spread, 0.0), axis=1, keepdims=True
@@ -384,13 +391,13 @@
             dma((3,)), dma((3,)),
             dma((CHUNKS, NSLOT)), dma((CHUNKS, NSLOT)),
             dma((NSLOT,)), dma((NSLOT,)),
-            dma((NROW,)), dma((NROW,)),
+            dma((4,)), dma((4,)),
             dma((NSLOT,)), dma((NSLOT,)),
             dma((16,)), dma((16,)),
             dma((16,)), dma((16,)),
         ],
         compiler_params=pltpu.CompilerParams(
-            has_side_effects=True, vmem_limit_bytes=60 * 2**20
+            collective_id=0, has_side_effects=True, vmem_limit_bytes=60 * 2**20
         ),
     )(
         orbital_factors.reshape(-1, naux), eps, occ_energy.astype(F32), jnp.asarray(weight_table()),

time: 132 us -> 110 us (0.83)
  Pallas kernels: 127 us -> 104 us
    pallas_call x1, Pallas kernels: 127 us -> 104 us  [on_device(): pl.pallas_call(kernel, out_shape=jax.ShapeDtypeStruct((16, 128), F32), in...]
where the time goes in v2:
time: 110 us; the launch traced here: 109 us
  Pallas kernels  104 us (95%)
  local copies, waits for them, and re-layouts  3.85 us (4%)
    pallas_call x1, Pallas kernels, on_device(): pl.pallas_call(kernel, out_shape=jax.ShapeDtypeStruct((16, 128), F32), in...  104 us

profile of v2, /device:TPU:1, one launch (start us, length us, event | category | flops | bytes accessed | tf_op | source)
XLA Modules:
  0.0 109.5 jit_solution(3637325797864492030)
XLA Ops:
  0.6 0.0 copy-start.1
  0.6 0.6 copy-done.1
  1.3 0.0 copy-start
  1.3 0.5 convert_element_type.7.occ_ref
  1.8 0.1 copy-done
  1.9 0.6 reshape_tile.3.eps_ref
  2.5 104.5 %shard_map.59 = f32[16,128]{1,0:T(8,128)} custom-call(bf16[64,6144]{1,0:T(8,128)(2,1)} %bitcast.3, f32[1,128]{1,0:T(1,128)} %reshape_tile.3.eps_ref, f32[8]{0:T(128)} %convert_element_type.7.occ_ref, f32[11,1,128]{2,1,0:T(1,128)} %constant.2.clone.weight_ref), custom_call_target="tpu_custom_call" | custom-call | tf_op jit(solution)/shard_map/pallas_call | solution.py:370
  107.0 1.2 %slice_bitcast_fusion = f32[8]{0:T(128)} fusion(f32[16,128]{1,0:T(8,128)} %shard_map.59), kind=kLoop, calls=%fused_computation | loop fusion | bytes 64 | tf_op jit(solution)/shard_map/squeeze | solution.py:405
  108.2 1.3 %slice.6 = f32[8,8]{1,0:T(8,128)} slice(f32[16,128]{1,0:T(8,128)} %shard_map.59), slice={[0:8], [0:8]} | slice | bytes 512 | tf_op jit(solution)/shard_map/slice | solution.py:405
  (1 shorter events, 0.0 us)
Async XLA Ops:
  0.6 0.7 copy-start.1
  1.3 0.7 copy-start

commit v3 on v2

--- a/solution.py
+++ b/solution.py
@@ -9,66 +9,70 @@
 from jax.sharding import PartitionSpec as P
 
 OFFSETS = (
-    (0, 1, 7),
+    (1, 0, 3),
+    (1, 0, 7),
+    (2, 2, 7),
     (0, 3, 7),
-    (1, 3, 3),
+    (3, 3, 7),
+    (2, 0, 7),
+    (0, 0, 3),
+    (1, 2, 7),
+    (0, 0, 7),
+    (0, 0, 2),
+    (0, 1, 1),
+    (0, 0, 1),
+    (0, 1, 0),
+    (0, 1, 2),
+    (0, 0, 0),
     (2, 3, 7),
-    (0, 0, 7),
-    (0, 2, 7),
-    (2, 2, 7),
-    (1, 0, 0),
-    (2, 0, 3),
-    (3, 0, 2),
-    (2, 0, 2),
-    (1, 3, 7),
-    (3, 0, 1),
-    (0, 0, 1),
-    (1, 0, 3),
-    (0, 0, 0),
 )
 COLS = 8
-ROW0 = 5
-NROW = 11
+ROW0 = 6
+NROW = 10
 FIRST = 0
 LAST = 5
 PLAN = (
-    (1, 0, 15, 0, 7), (1, 0, 15, 4, 13), (1, 0, 15, 5, 4), (1, 1, 15, 0, 7), (1, 1, 15, 4, 13), (1, 1, 15, 5, 4),
-    (1, 2, 15, 0, 7), (1, 2, 15, 4, 13), (1, 2, 15, 5, 4), (0, 0, 4, 0, 0), (0, 0, 7, 0, 0), (0, 0, 13, 0, 0),
-    (1, 0, 4, 2, 0), (1, 0, 4, 3, 1), (1, 0, 13, 1, 12), (1, 3, 15, 0, 7), (1, 3, 15, 4, 13), (1, 3, 15, 5, 4),
-    (0, 1, 4, 0, 0), (0, 1, 7, 0, 0), (0, 1, 13, 0, 0), (1, 1, 4, 2, 0), (1, 1, 4, 3, 1), (1, 1, 13, 1, 12),
-    (1, 4, 15, 5, 4), (0, 0, 0, 0, 0), (0, 0, 1, 0, 0), (0, 0, 12, 0, 0), (1, 0, 0, 2, 5), (1, 0, 1, 0, 11),
-    (1, 0, 12, 4, 9), (0, 2, 4, 0, 0), (0, 2, 7, 0, 0), (0, 2, 13, 0, 0), (1, 2, 4, 2, 0), (1, 2, 4, 3, 1),
-    (1, 2, 13, 1, 12), (1, 5, 15, 5, 4), (0, 1, 0, 0, 0), (0, 1, 1, 0, 0), (0, 1, 12, 0, 0), (1, 1, 1, 0, 11),
-    (1, 1, 12, 4, 9), (1, 1, 0, 2, 5), (0, 3, 4, 0, 0), (0, 3, 7, 0, 0), (0, 3, 13, 0, 0), (1, 3, 4, 3, 1),
-    (1, 3, 13, 1, 12), (1, 4, 15, 4, 13), (0, 0, 5, 0, 0), (0, 2, 1, 0, 0), (0, 2, 12, 0, 0), (1, 3, 4, 2, 0),
-    (0, 0, 9, 0, 0), (0, 0, 11, 0, 0), (0, 4, 4, 0, 0), (1, 0, 9, 1, 10), (1, 0, 11, 0, 3), (1, 4, 4, 3, 1),
-    (1, 2, 1, 0, 11), (1, 2, 12, 4, 9), (0, 2, 0, 0, 0), (0, 3, 1, 0, 0), (0, 3, 12, 0, 0), (1, 2, 0, 2, 5),
-    (0, 1, 9, 0, 0), (0, 1, 11, 0, 0), (0, 5, 4, 0, 0), (1, 1, 9, 1, 10), (1, 5, 4, 3, 1), (1, 1, 11, 0, 3),
-    (1, 5, 15, 4, 13), (0, 0, 10, 0, 0), (0, 1, 5, 0, 0), (0, 4, 1, 0, 0), (1, 4, 4, 2, 0), (0, 0, 3, 0, 0),
-    (0, 4, 13, 0, 0), (1, 0, 3, 3, 6), (1, 4, 13, 1, 12), (1, 0, 10, 4, 8), (1, 3, 1, 0, 11), (0, 1, 10, 0, 0),
-    (0, 3, 0, 0, 0), (0, 5, 1, 0, 0), (1, 3, 0, 2, 5), (0, 2, 9, 0, 0), (0, 2, 11, 0, 0), (1, 2, 9, 1, 10),
-    (1, 2, 11, 0, 3), (1, 3, 12, 4, 9), (0, 0, 6, 0, 0), (0, 2, 5, 0, 0), (0, 4, 12, 0, 0), (1, 5, 4, 2, 0),
-    (0, 1, 3, 0, 0), (0, 5, 13, 0, 0), (1, 1, 3, 3, 6), (1, 5, 13, 1, 12), (1, 1, 10, 4, 8), (1, 4, 1, 0, 11),
-    (0, 2, 10, 0, 0), (0, 4, 0, 0, 0), (1, 4, 0, 2, 5), (0, 0, 8, 0, 0), (0, 3, 11, 0, 0), (1, 0, 8, 1, 14),
-    (1, 3, 11, 0, 3), (1, 4, 12, 4, 9), (0, 1, 6, 0, 0), (0, 3, 5, 0, 0), (0, 5, 12, 0, 0), (0, 2, 3, 0, 0),
-    (0, 3, 9, 0, 0), (1, 2, 3, 3, 6), (1, 3, 9, 1, 10), (1, 2, 10, 4, 8), (1, 5, 1, 0, 11), (0, 0, 14, 0, 0),
-    (0, 5, 0, 0, 0), (1, 0, 14, 3, 2), (1, 5, 0, 2, 5), (0, 1, 8, 0, 0), (0, 4, 11, 0, 0), (1, 1, 8, 1, 14),
-    (1, 4, 11, 0, 3), (1, 5, 12, 4, 9), (0, 2, 6, 0, 0), (0, 3, 10, 0, 0), (0, 4, 5, 0, 0), (0, 3, 3, 0, 0),
-    (0, 4, 9, 0, 0), (1, 3, 3, 3, 6), (1, 4, 9, 1, 10), (1, 3, 10, 4, 8), (0, 0, 2, 0, 0), (0, 1, 14, 0, 0),
-    (0, 5, 5, 0, 0), (1, 1, 14, 3, 2), (0, 2, 8, 0, 0), (0, 5, 11, 0, 0), (1, 2, 8, 1, 14), (1, 5, 11, 0, 3),
-    (1, 4, 15, 0, 7), (0, 3, 6, 0, 0), (0, 4, 10, 0, 0), (1, 4, 10, 4, 8), (0, 4, 3, 0, 0), (0, 5, 9, 0, 0),
-    (1, 4, 3, 3, 6), (1, 5, 9, 1, 10), (1, 5, 15, 0, 7), (0, 1, 2, 0, 0), (0, 2, 14, 0, 0), (1, 2, 14, 3, 2),
-    (0, 3, 8, 0, 0), (0, 5, 3, 0, 0), (1, 3, 8, 1, 14), (1, 5, 3, 3, 6), (0, 4, 6, 0, 0), (0, 5, 10, 0, 0),
-    (1, 5, 10, 4, 8), (0, 4, 7, 0, 0), (0, 4, 8, 0, 0), (1, 4, 8, 1, 14), (0, 2, 2, 0, 0), (0, 3, 14, 0, 0),
-    (1, 3, 14, 3, 2), (0, 5, 7, 0, 0), (0, 5, 8, 0, 0), (1, 5, 8, 1, 14), (0, 4, 14, 0, 0), (0, 5, 6, 0, 0),
-    (1, 4, 14, 3, 2), (0, 3, 2, 0, 0), (0, 5, 14, 0, 0), (1, 5, 14, 3, 2), (0, 4, 2, 0, 0), (0, 5, 2, 0, 0),
+    (1, 0, 14, 2, 12), (1, 0, 14, 4, 11), (1, 0, 14, 5, 8), (1, 1, 14, 2, 12), (1, 1, 14, 4, 11), (1, 1, 14, 5, 8),
+    (0, 0, 8, 0, 0), (0, 0, 11, 0, 0), (0, 0, 12, 0, 0), (1, 0, 8, 0, 1), (1, 0, 8, 3, 3), (1, 0, 11, 2, 10),
+    (1, 0, 11, 4, 9), (1, 2, 14, 5, 8), (0, 1, 8, 0, 0), (0, 1, 11, 0, 0), (0, 1, 12, 0, 0), (1, 1, 8, 0, 1),
+    (1, 1, 8, 3, 3), (1, 1, 11, 2, 10), (1, 2, 14, 4, 11), (1, 3, 14, 5, 8), (0, 0, 1, 0, 0), (0, 0, 3, 0, 0),
+    (1, 0, 3, 1, 4), (0, 0, 9, 0, 0), (0, 0, 10, 0, 0), (0, 2, 8, 0, 0), (1, 0, 1, 0, 5), (1, 2, 8, 3, 3),
+    (1, 0, 9, 2, 13), (1, 1, 11, 4, 9), (1, 4, 14, 5, 8), (0, 1, 1, 0, 0), (0, 1, 3, 0, 0), (1, 1, 3, 1, 4),
+    (0, 1, 10, 0, 0), (0, 2, 11, 0, 0), (0, 3, 8, 0, 0), (1, 1, 1, 0, 5), (1, 3, 8, 3, 3), (1, 0, 9, 4, 6),
+    (1, 2, 14, 2, 12), (1, 5, 14, 5, 8), (0, 0, 4, 0, 0), (0, 0, 5, 0, 0), (0, 2, 3, 0, 0), (1, 0, 4, 1, 15),
+    (0, 0, 13, 0, 0), (0, 1, 9, 0, 0), (0, 4, 8, 0, 0), (1, 3, 8, 0, 1), (1, 4, 8, 3, 3), (1, 1, 9, 2, 13),
+    (1, 3, 14, 4, 11), (0, 1, 4, 0, 0), (0, 1, 5, 0, 0), (0, 3, 3, 0, 0), (1, 2, 3, 1, 4), (0, 0, 6, 0, 0),
+    (0, 2, 12, 0, 0), (0, 5, 8, 0, 0), (1, 1, 5, 3, 15), (1, 4, 8, 0, 1), (1, 2, 11, 2, 10), (1, 2, 11, 4, 9),
+    (0, 0, 15, 0, 0), (0, 3, 1, 0, 0), (0, 4, 3, 0, 0), (1, 3, 3, 1, 4), (0, 1, 13, 0, 0), (0, 3, 11, 0, 0),
+    (1, 0, 15, 3, 2), (1, 3, 1, 0, 5), (1, 1, 9, 4, 6), (1, 3, 11, 2, 10), (0, 2, 4, 0, 0), (0, 1, 15, 0, 0),
+    (0, 4, 1, 0, 0), (1, 2, 4, 1, 15), (0, 2, 9, 0, 0), (0, 2, 10, 0, 0), (1, 0, 6, 0, 0), (1, 1, 15, 3, 2),
+    (1, 2, 9, 2, 13), (1, 4, 14, 4, 11), (0, 3, 4, 0, 0), (0, 0, 2, 0, 0), (0, 3, 5, 0, 0), (1, 0, 2, 1, 7),
+    (0, 1, 6, 0, 0), (0, 3, 10, 0, 0), (1, 3, 10, 5, 12), (1, 4, 1, 0, 5), (1, 5, 8, 3, 3), (1, 3, 11, 4, 9),
+    (1, 4, 14, 2, 12), (0, 2, 15, 0, 0), (0, 0, 0, 0, 0), (0, 1, 2, 0, 0), (1, 1, 2, 1, 7), (0, 2, 13, 0, 0),
+    (0, 4, 11, 0, 0), (1, 2, 8, 0, 1), (1, 3, 5, 3, 15), (1, 2, 9, 4, 6), (1, 4, 11, 2, 10), (0, 0, 7, 0, 0),
+    (0, 3, 12, 0, 0), (0, 4, 5, 0, 0), (0, 5, 3, 0, 0), (1, 5, 3, 1, 4), (0, 3, 9, 0, 0), (0, 4, 12, 0, 0),
+    (1, 1, 6, 0, 0), (1, 2, 15, 3, 2), (1, 3, 9, 2, 13), (1, 5, 14, 4, 11), (0, 1, 7, 0, 0), (0, 2, 1, 0, 0),
+    (0, 3, 15, 0, 0), (1, 4, 3, 1, 4), (0, 2, 6, 0, 0), (0, 4, 10, 0, 0), (1, 2, 1, 0, 5), (1, 4, 5, 3, 15),
+    (1, 4, 11, 4, 9), (1, 5, 14, 2, 12), (0, 5, 4, 0, 0), (0, 1, 0, 0, 0), (0, 2, 2, 0, 0), (1, 2, 2, 1, 7),
+    (0, 3, 13, 0, 0), (0, 5, 11, 0, 0), (1, 2, 6, 0, 0), (1, 3, 15, 3, 2), (1, 3, 9, 4, 6), (1, 5, 11, 2, 10),
+    (0, 4, 4, 0, 0), (0, 2, 5, 0, 0), (0, 4, 15, 0, 0), (1, 5, 4, 1, 15), (0, 4, 9, 0, 0), (0, 5, 12, 0, 0),
+    (1, 4, 15, 3, 2), (1, 5, 8, 0, 1), (1, 4, 9, 2, 13), (1, 5, 11, 4, 9), (0, 2, 7, 0, 0), (0, 2, 0, 0, 0),
+    (0, 3, 2, 0, 0), (1, 3, 2, 1, 7), (0, 3, 6, 0, 0), (0, 5, 10, 0, 0), (1, 3, 6, 0, 0), (1, 4, 9, 4, 6),
+    (0, 5, 15, 0, 0), (1, 5, 15, 3, 2), (0, 4, 2, 0, 0), (0, 5, 1, 0, 0), (1, 4, 2, 1, 7), (0, 4, 13, 0, 0),
+    (0, 5, 9, 0, 0), (1, 5, 1, 0, 5), (1, 5, 9, 2, 13), (1, 5, 9, 4, 6), (0, 3, 7, 0, 0), (0, 3, 0, 0, 0),
+    (0, 4, 6, 0, 0), (1, 4, 6, 0, 0), (0, 5, 2, 0, 0), (1, 5, 2, 1, 7), (0, 4, 7, 0, 0), (0, 5, 5, 0, 0),
+    (0, 5, 13, 0, 0), (0, 5, 6, 0, 0), (1, 5, 6, 0, 0), (0, 4, 0, 0, 0), (0, 5, 7, 0, 0), (0, 5, 0, 0, 0),
 )
 
 
 NSLOT = len(OFFSETS)
 CHUNKS = 1 + max(item[1] for item in PLAN)
 OWN = OFFSETS.index((0, 0, 0))
-STEPS = ((1, 0, 0), (3, 0, 0), (0, 1, 0), (0, 3, 0), (0, 0, 1), (0, 0, 7))
+STEPS = (
+    (1, 0, 0), (3, 0, 0), (0, 1, 0), (0, 3, 0), (0, 0, 1), (0, 0, 7),
+    (0, 0, 2), (0, 0, 6), (0, 0, 3), (0, 0, 5),
+)
+EPS_CHUNK = CHUNKS // 2
 SIDES = (4, 4, 8)
 MESH = pl.DeviceIdType.MESH
 NI = 8
@@ -135,12 +139,8 @@
         ).wait_recv()
 
     peers = {(0, 0, 0, 1)}
-    for offset in OFFSETS:
-        peers |= {offset + (0,), difference((0, 0, 0), offset) + (0,)}
-    peers |= {step + (0,) for step in STEPS}
-    peers |= {(m // 4, m % 4, 0, 0) for m in range(16)}
-    peers |= {(0, 0, m // 2, m % 2) for m in range(16)}
-    peers -= {(0, 0, 0, 0)}
+    for step in {item[3] for item in PLAN if item[0] == 1}:
+        peers |= {STEPS[step] + (0,), difference((0, 0, 0), STEPS[step]) + (0,)}
     barrier = pltpu.get_barrier_semaphore()
     for peer in sorted(peers):
         pl.semaphore_signal(
@@ -206,21 +206,16 @@
     def eps_exchange():
         arrived(epspart, part_send.at[1], part_recv.at[1], partner)
         epsbuf[OWN] = jnp.where((lane // 8) % 2 == core, eps_ref[...], epspart[...])
-        for slot in range(NSLOT):
-            if slot != OWN:
-                send(
-                    epsbuf.at[OWN], epsbuf.at[slot], eps_send.at[slot], eps_recv.at[slot],
-                    device(OFFSETS[slot], core),
-                )
 
     left_in = [NSLOT - 1] * CHUNKS
     queue = []
-    sent = 0
     for kind, chunk, slot, step, target in PLAN:
         if kind == 0:
             arrived(
                 buf.at[chunk, slot], ring_send.at[chunk, slot], ring_recv.at[chunk, slot], partner
             )
+            if chunk == EPS_CHUNK:
+                arrived(epsbuf.at[slot], eps_send.at[slot], eps_recv.at[slot], partner)
             left_in[chunk] -= 1
             if queue:
                 multiply(*queue.pop(0))
@@ -228,15 +223,19 @@
                 queue += [(chunk, block) for block in range(4)]
         else:
             if slot == OWN:
+                if chunk == EPS_CHUNK and chunk not in ready:
+                    eps_exchange()
                 prepare(chunk)
             send(
                 buf.at[chunk, slot], buf.at[chunk, target],
                 ring_send.at[chunk, target], ring_recv.at[chunk, target],
                 device(STEPS[step], core),
             )
-            sent += 1
-            if sent == 12:
-                eps_exchange()
+            if chunk == EPS_CHUNK:
+                send(
+                    epsbuf.at[slot], epsbuf.at[target], eps_send.at[target],
+                    eps_recv.at[target], device(STEPS[step], core),
+                )
 
     for chunk, block in queue:
         multiply(chunk, block)
@@ -247,9 +246,6 @@
                 acc_send.at[block], acc_recv.at[block], partner,
             )
 
-    for slot in range(NSLOT):
-        if slot != OWN:
-            arrived(epsbuf.at[slot], eps_send.at[slot], eps_recv.at[slot], partner)
     virt_col = jnp.zeros((1, 128), F32)
     for slot in range(COLS):
         virt_col = jnp.where(lane // 16 == slot, epsbuf[slot], virt_col)

time: 110 us -> 99.4 us (0.904)
  Pallas kernels: 104 us -> 94.1 us
    pallas_call x1, Pallas kernels: 104 us -> 94.1 us  [on_device(): pl.pallas_call(kernel, out_shape=jax.ShapeDtypeStruct((16, 128), F32), in...]
where the time goes in v3:
time: 99.4 us; the launch traced here: 99.1 us
  Pallas kernels  94.1 us (95%)
  local copies, waits for them, and re-layouts  3.85 us (4%)
    pallas_call x1, Pallas kernels, on_device(): pl.pallas_call(kernel, out_shape=jax.ShapeDtypeStruct((16, 128), F32), in...  94.1 us

profile of v3, /device:TPU:1, one launch (start us, length us, event | category | flops | bytes accessed | tf_op | source)
XLA Modules:
  0.0 99.1 jit_solution(3766322379011164970)
XLA Ops:
  0.6 0.0 copy-start.1
  0.6 0.6 copy-done.1
  1.3 0.0 copy-start
  1.3 0.5 convert_element_type.7.occ_ref
  1.8 0.1 copy-done
  1.9 0.6 reshape_tile.3.eps_ref
  2.5 94.1 %shard_map.59 = f32[16,128]{1,0:T(8,128)} custom-call(bf16[64,6144]{1,0:T(8,128)(2,1)} %bitcast.3, f32[1,128]{1,0:T(1,128)} %reshape_tile.3.eps_ref, f32[8]{0:T(128)} %convert_element_type.7.occ_ref, f32[10,1,128]{2,1,0:T(1,128)} %constant.2.clone.weight_ref), custom_call_target="tpu_custom_call" | custom-call | tf_op jit(solution)/shard_map/pallas_call | solution.py:366
  96.7 1.2 %slice_bitcast_fusion = f32[8]{0:T(128)} fusion(f32[16,128]{1,0:T(8,128)} %shard_map.59), kind=kLoop, calls=%fused_computation | loop fusion | bytes 64 | tf_op jit(solution)/shard_map/squeeze | solution.py:401
  97.9 1.3 %slice.6 = f32[8,8]{1,0:T(8,128)} slice(f32[16,128]{1,0:T(8,128)} %shard_map.59), slice={[0:8], [0:8]} | slice | bytes 512 | tf_op jit(solution)/shard_map/slice | solution.py:401
  (1 shorter events, 0.0 us)
Async XLA Ops:
  0.6 0.7 copy-start.1
  1.3 0.7 copy-start

commit v4 on v3

--- a/solution.py
+++ b/solution.py
@@ -9,59 +9,49 @@
 from jax.sharding import PartitionSpec as P
 
 OFFSETS = (
-    (1, 0, 3),
-    (1, 0, 7),
-    (2, 2, 7),
-    (0, 3, 7),
-    (3, 3, 7),
-    (2, 0, 7),
-    (0, 0, 3),
-    (1, 2, 7),
+    (0, 3, 1),
+    (2, 0, 1),
+    (1, 3, 1),
+    (3, 0, 5),
+    (3, 0, 1),
+    (2, 2, 1),
+    (3, 2, 1),
+    (0, 0, 5),
+    (0, 0, 0),
+    (0, 1, 6),
+    (2, 3, 1),
+    (0, 1, 0),
+    (0, 1, 7),
     (0, 0, 7),
-    (0, 0, 2),
-    (0, 1, 1),
     (0, 0, 1),
-    (0, 1, 0),
-    (0, 1, 2),
-    (0, 0, 0),
-    (2, 3, 7),
+    (0, 0, 6),
 )
 COLS = 8
 ROW0 = 6
 NROW = 10
 FIRST = 0
-LAST = 5
+LAST = 3
 PLAN = (
-    (1, 0, 14, 2, 12), (1, 0, 14, 4, 11), (1, 0, 14, 5, 8), (1, 1, 14, 2, 12), (1, 1, 14, 4, 11), (1, 1, 14, 5, 8),
-    (0, 0, 8, 0, 0), (0, 0, 11, 0, 0), (0, 0, 12, 0, 0), (1, 0, 8, 0, 1), (1, 0, 8, 3, 3), (1, 0, 11, 2, 10),
-    (1, 0, 11, 4, 9), (1, 2, 14, 5, 8), (0, 1, 8, 0, 0), (0, 1, 11, 0, 0), (0, 1, 12, 0, 0), (1, 1, 8, 0, 1),
-    (1, 1, 8, 3, 3), (1, 1, 11, 2, 10), (1, 2, 14, 4, 11), (1, 3, 14, 5, 8), (0, 0, 1, 0, 0), (0, 0, 3, 0, 0),
-    (1, 0, 3, 1, 4), (0, 0, 9, 0, 0), (0, 0, 10, 0, 0), (0, 2, 8, 0, 0), (1, 0, 1, 0, 5), (1, 2, 8, 3, 3),
-    (1, 0, 9, 2, 13), (1, 1, 11, 4, 9), (1, 4, 14, 5, 8), (0, 1, 1, 0, 0), (0, 1, 3, 0, 0), (1, 1, 3, 1, 4),
-    (0, 1, 10, 0, 0), (0, 2, 11, 0, 0), (0, 3, 8, 0, 0), (1, 1, 1, 0, 5), (1, 3, 8, 3, 3), (1, 0, 9, 4, 6),
-    (1, 2, 14, 2, 12), (1, 5, 14, 5, 8), (0, 0, 4, 0, 0), (0, 0, 5, 0, 0), (0, 2, 3, 0, 0), (1, 0, 4, 1, 15),
-    (0, 0, 13, 0, 0), (0, 1, 9, 0, 0), (0, 4, 8, 0, 0), (1, 3, 8, 0, 1), (1, 4, 8, 3, 3), (1, 1, 9, 2, 13),
-    (1, 3, 14, 4, 11), (0, 1, 4, 0, 0), (0, 1, 5, 0, 0), (0, 3, 3, 0, 0), (1, 2, 3, 1, 4), (0, 0, 6, 0, 0),
-    (0, 2, 12, 0, 0), (0, 5, 8, 0, 0), (1, 1, 5, 3, 15), (1, 4, 8, 0, 1), (1, 2, 11, 2, 10), (1, 2, 11, 4, 9),
-    (0, 0, 15, 0, 0), (0, 3, 1, 0, 0), (0, 4, 3, 0, 0), (1, 3, 3, 1, 4), (0, 1, 13, 0, 0), (0, 3, 11, 0, 0),
-    (1, 0, 15, 3, 2), (1, 3, 1, 0, 5), (1, 1, 9, 4, 6), (1, 3, 11, 2, 10), (0, 2, 4, 0, 0), (0, 1, 15, 0, 0),
-    (0, 4, 1, 0, 0), (1, 2, 4, 1, 15), (0, 2, 9, 0, 0), (0, 2, 10, 0, 0), (1, 0, 6, 0, 0), (1, 1, 15, 3, 2),
-    (1, 2, 9, 2, 13), (1, 4, 14, 4, 11), (0, 3, 4, 0, 0), (0, 0, 2, 0, 0), (0, 3, 5, 0, 0), (1, 0, 2, 1, 7),
-    (0, 1, 6, 0, 0), (0, 3, 10, 0, 0), (1, 3, 10, 5, 12), (1, 4, 1, 0, 5), (1, 5, 8, 3, 3), (1, 3, 11, 4, 9),
-    (1, 4, 14, 2, 12), (0, 2, 15, 0, 0), (0, 0, 0, 0, 0), (0, 1, 2, 0, 0), (1, 1, 2, 1, 7), (0, 2, 13, 0, 0),
-    (0, 4, 11, 0, 0), (1, 2, 8, 0, 1), (1, 3, 5, 3, 15), (1, 2, 9, 4, 6), (1, 4, 11, 2, 10), (0, 0, 7, 0, 0),
-    (0, 3, 12, 0, 0), (0, 4, 5, 0, 0), (0, 5, 3, 0, 0), (1, 5, 3, 1, 4), (0, 3, 9, 0, 0), (0, 4, 12, 0, 0),
-    (1, 1, 6, 0, 0), (1, 2, 15, 3, 2), (1, 3, 9, 2, 13), (1, 5, 14, 4, 11), (0, 1, 7, 0, 0), (0, 2, 1, 0, 0),
-    (0, 3, 15, 0, 0), (1, 4, 3, 1, 4), (0, 2, 6, 0, 0), (0, 4, 10, 0, 0), (1, 2, 1, 0, 5), (1, 4, 5, 3, 15),
-    (1, 4, 11, 4, 9), (1, 5, 14, 2, 12), (0, 5, 4, 0, 0), (0, 1, 0, 0, 0), (0, 2, 2, 0, 0), (1, 2, 2, 1, 7),
-    (0, 3, 13, 0, 0), (0, 5, 11, 0, 0), (1, 2, 6, 0, 0), (1, 3, 15, 3, 2), (1, 3, 9, 4, 6), (1, 5, 11, 2, 10),
-    (0, 4, 4, 0, 0), (0, 2, 5, 0, 0), (0, 4, 15, 0, 0), (1, 5, 4, 1, 15), (0, 4, 9, 0, 0), (0, 5, 12, 0, 0),
-    (1, 4, 15, 3, 2), (1, 5, 8, 0, 1), (1, 4, 9, 2, 13), (1, 5, 11, 4, 9), (0, 2, 7, 0, 0), (0, 2, 0, 0, 0),
-    (0, 3, 2, 0, 0), (1, 3, 2, 1, 7), (0, 3, 6, 0, 0), (0, 5, 10, 0, 0), (1, 3, 6, 0, 0), (1, 4, 9, 4, 6),
-    (0, 5, 15, 0, 0), (1, 5, 15, 3, 2), (0, 4, 2, 0, 0), (0, 5, 1, 0, 0), (1, 4, 2, 1, 7), (0, 4, 13, 0, 0),
-    (0, 5, 9, 0, 0), (1, 5, 1, 0, 5), (1, 5, 9, 2, 13), (1, 5, 9, 4, 6), (0, 3, 7, 0, 0), (0, 3, 0, 0, 0),
-    (0, 4, 6, 0, 0), (1, 4, 6, 0, 0), (0, 5, 2, 0, 0), (1, 5, 2, 1, 7), (0, 4, 7, 0, 0), (0, 5, 5, 0, 0),
-    (0, 5, 13, 0, 0), (0, 5, 6, 0, 0), (1, 5, 6, 0, 0), (0, 4, 0, 0, 0), (0, 5, 7, 0, 0), (0, 5, 0, 0, 0),
+    (1, 0, 8, 4, 14), (1, 0, 8, 5, 13), (1, 2, 8, 2, 11), (1, 1, 8, 4, 14), (1, 1, 8, 5, 13), (1, 3, 8, 2, 11),
+    (0, 0, 13, 0, 0), (0, 0, 14, 0, 0), (1, 0, 14, 1, 4), (1, 0, 14, 3, 0), (0, 2, 11, 0, 0), (1, 0, 13, 5, 15),
+    (1, 2, 8, 4, 14), (0, 1, 13, 0, 0), (0, 1, 14, 0, 0), (1, 1, 14, 1, 4), (1, 1, 14, 3, 0), (0, 3, 11, 0, 0),
+    (0, 0, 0, 0, 0), (0, 0, 4, 0, 0), (1, 0, 0, 0, 2), (1, 1, 13, 5, 15), (1, 3, 8, 4, 14), (0, 0, 15, 0, 0),
+    (0, 2, 14, 0, 0), (1, 0, 4, 1, 1), (1, 0, 15, 2, 9), (1, 2, 14, 3, 0), (0, 1, 0, 0, 0), (0, 1, 4, 0, 0),
+    (1, 1, 0, 0, 2), (1, 2, 8, 5, 13), (0, 0, 2, 0, 0), (0, 1, 15, 0, 0), (0, 3, 14, 0, 0), (1, 1, 4, 1, 1),
+    (1, 1, 15, 2, 9), (1, 3, 14, 3, 0), (0, 0, 1, 0, 0), (0, 0, 9, 0, 0), (0, 2, 0, 0, 0), (1, 0, 9, 4, 12),
+    (1, 2, 0, 0, 2), (1, 0, 15, 5, 7), (0, 1, 2, 0, 0), (0, 2, 13, 0, 0), (1, 0, 1, 3, 10), (1, 3, 14, 1, 4),
+    (0, 1, 1, 0, 0), (0, 1, 9, 0, 0), (0, 3, 0, 0, 0), (1, 1, 9, 4, 12), (1, 3, 0, 0, 2), (1, 3, 8, 5, 13),
+    (0, 0, 12, 0, 0), (0, 2, 2, 0, 0), (0, 0, 7, 0, 0), (1, 0, 7, 1, 3), (1, 1, 1, 3, 10), (0, 0, 10, 0, 0),
+    (0, 3, 4, 0, 0), (1, 0, 12, 4, 11), (1, 2, 2, 0, 10), (1, 2, 13, 5, 15), (0, 1, 12, 0, 0), (0, 3, 2, 0, 0),
+    (0, 3, 13, 0, 0), (1, 0, 10, 3, 5), (1, 2, 14, 1, 4), (0, 0, 3, 0, 0), (0, 1, 10, 0, 0), (1, 1, 12, 4, 11),
+    (1, 3, 2, 0, 10), (1, 1, 15, 5, 7), (0, 0, 11, 0, 0), (0, 2, 10, 0, 0), (1, 2, 10, 2, 1), (0, 2, 15, 0, 0),
+    (1, 1, 10, 3, 5), (1, 3, 4, 1, 1), (0, 0, 5, 0, 0), (0, 2, 4, 0, 0), (1, 0, 5, 0, 6), (1, 3, 13, 5, 15),
+    (0, 1, 11, 0, 0), (0, 3, 10, 0, 0), (1, 2, 15, 2, 9), (0, 1, 7, 0, 0), (1, 1, 7, 1, 3), (1, 2, 10, 3, 5),
+    (0, 2, 1, 0, 0), (0, 1, 5, 0, 0), (0, 3, 1, 0, 0), (1, 1, 5, 0, 6), (1, 2, 15, 5, 7), (0, 0, 6, 0, 0),
+    (0, 3, 15, 0, 0), (1, 3, 10, 3, 5), (1, 3, 15, 2, 9), (0, 2, 9, 0, 0), (1, 2, 9, 4, 12), (0, 1, 3, 0, 0),
+    (0, 2, 5, 0, 0), (1, 2, 5, 0, 6), (1, 3, 15, 5, 7), (0, 1, 6, 0, 0), (0, 2, 7, 0, 0), (1, 2, 7, 1, 3),
+    (0, 3, 5, 0, 0), (0, 3, 9, 0, 0), (1, 3, 5, 0, 6), (1, 3, 11, 5, 12), (0, 2, 12, 0, 0), (0, 2, 6, 0, 0),
+    (0, 3, 7, 0, 0), (1, 3, 7, 1, 3), (0, 2, 3, 0, 0), (0, 3, 6, 0, 0), (0, 3, 12, 0, 0), (0, 3, 3, 0, 0),
 )
 
 
@@ -100,7 +90,7 @@
 
 
 def kernel(
-    x_ref, eps_ref, occ_ref, weight_ref, out_ref,
+    x_ref, eps_ref, occ_ref, weight_ref, pair_ref, virt_ref,
     raw, buf, acc, accr, epsbuf, epspart, pair_acc, square, vsrc, vrecv, csrc, crecv,
     plane, line,
     in_sem, part_send, part_recv, ring_send, ring_recv, eps_send, eps_recv,
@@ -153,14 +143,23 @@
     width = half // CHUNKS
     mine = pl.ds(pl.multiple_of(core * 64, 64), 64)
     theirs = pl.ds(pl.multiple_of(other * 64, 64), 64)
-    local = pltpu.make_async_copy(
-        x_ref.at[:, pl.ds(pl.multiple_of(core * half, 128), half)], raw.at[mine], in_sem
-    )
-    send(
-        x_ref.at[:, pl.ds(pl.multiple_of(other * half, 128), half)], raw.at[mine],
-        part_send.at[0], part_recv.at[0], partner,
-    )
-    local.start()
+    parts = ((0, width), (width, half - width))
+    for index, (start, size) in enumerate(parts):
+        send(
+            x_ref.at[:, pl.ds(pl.multiple_of(other * half + start, 128), size)],
+            raw.at[mine, pl.ds(start, size)],
+            part_send.at[3 * index], part_recv.at[3 * index], partner,
+        )
+    local = [
+        pltpu.make_async_copy(
+            x_ref.at[:, pl.ds(pl.multiple_of(core * half + start, 128), size)],
+            raw.at[mine, pl.ds(start, size)],
+            in_sem.at[index],
+        )
+        for index, (start, size) in enumerate(parts)
+    ]
+    for copy in local:
+        copy.start()
     send(eps_ref, epspart, part_send.at[1], part_recv.at[1], partner)
 
     lane = lax.broadcasted_iota(jnp.int32, (1, 128), 1)
@@ -170,19 +169,27 @@
     source = lax.broadcasted_iota(jnp.int32, (128, 128), 1)
     order = (source == ((to // 8) % 2) * 64 + (to % 8) * 8 + to // 16).astype(F32).astype(jnp.bfloat16)
 
-    local.wait()
-    arrived(raw.at[theirs], part_send.at[0], part_recv.at[0], partner)
+    def take(index):
+        start, size = parts[index]
+        local[index].wait()
+        arrived(
+            raw.at[theirs, pl.ds(start, size)], part_send.at[3 * index], part_recv.at[3 * index],
+            partner,
+        )
 
     ready = set()
 
     def prepare(chunk):
         if chunk in ready:
             return
+        if len(ready) < 2:
+            take(len(ready))
+        assert ready or chunk == 0
         ready.add(chunk)
         piece = raw[:, chunk * width : (chunk + 1) * width]
         buf[chunk, OWN] = jnp.dot(order, piece, preferred_element_type=F32).astype(jnp.bfloat16)
 
-    def multiply(chunk, block):
+    def multiply(chunk, block, groups):
         right = jnp.concatenate(
             [
                 buf[chunk, 0:COLS, 16 * j : 16 * j + 16, :].reshape(COLS * 16, width)
@@ -191,8 +198,7 @@
             axis=0,
         )
         lanes = slice(256 * block, 256 * block + 256)
-        for k in range(0, NROW, GROUP):
-            count = min(GROUP, NROW - k)
+        for k, count in groups:
             left = buf[chunk, ROW0 + k : ROW0 + k + count].reshape(count * 128, width)
             part = lax.dot_general(
                 left, right, (((1,), (1,)), ((), ())), preferred_element_type=F32
@@ -202,6 +208,8 @@
                     acc[k : k + count, h, :, :, lanes] = part[:, :, h]
                 else:
                     acc[k : k + count, h, :, :, lanes] += part[:, :, h]
+
+    groups = [(k, min(GROUP, NROW - k)) for k in range(0, NROW, GROUP)]
 
     def eps_exchange():
         arrived(epspart, part_send.at[1], part_recv.at[1], partner)
@@ -218,7 +226,7 @@
                 arrived(epsbuf.at[slot], eps_send.at[slot], eps_recv.at[slot], partner)
             left_in[chunk] -= 1
             if queue:
-                multiply(*queue.pop(0))
+                multiply(*queue.pop(0), groups)
             if left_in[chunk] == 0:
                 queue += [(chunk, block) for block in range(4)]
         else:
@@ -238,13 +246,15 @@
                 )
 
     for chunk, block in queue:
-        multiply(chunk, block)
-        if chunk == LAST:
-            lanes = slice(256 * block, 256 * block + 256)
-            send(
-                acc.at[:, other, :, :, lanes], accr.at[:, :, :, lanes],
-                acc_send.at[block], acc_recv.at[block], partner,
-            )
+        if chunk != LAST:
+            multiply(chunk, block, groups)
+    for index, (k, count) in enumerate(groups):
+        for block in range(4):
+            multiply(LAST, block, [(k, count)])
+        send(
+            acc.at[k : k + count, other], accr.at[k : k + count],
+            acc_send.at[index], acc_recv.at[index], partner,
+        )
 
     virt_col = jnp.zeros((1, 128), F32)
     for slot in range(COLS):
@@ -252,10 +262,6 @@
     virt_col = jnp.broadcast_to(virt_col, (8, 128))
     pair_acc[...] = jnp.zeros_like(pair_acc)
     square[...] = jnp.zeros_like(square)
-
-    for block in range(4):
-        lanes = slice(256 * block, 256 * block + 256)
-        arrived(accr.at[:, :, :, lanes], acc_send.at[block], acc_recv.at[block], partner)
 
     def energy(k, col_sum):
         spread = jnp.broadcast_to(epsbuf[ROW0 + k], (8, 128))
@@ -284,7 +290,10 @@
         square[pl.ds(pl.multiple_of(k * 8, 8), 8), :] = total
         return col_sum + total
 
-    col_sum = lax.fori_loop(0, NROW, energy, jnp.zeros((8, 128), F32))
+    col_sum = jnp.zeros((8, 128), F32)
+    for index, (k, count) in enumerate(groups):
+        arrived(accr.at[k : k + count], acc_send.at[index], acc_recv.at[index], partner)
+        col_sum = lax.fori_loop(k, k + count, energy, col_sum)
     vsrc[:, 0:128] = jnp.sum(square[...].T, axis=0, keepdims=True)
     vsrc[:, 128:256] = jnp.sum(col_sum, axis=0, keepdims=True)
 
@@ -346,13 +355,13 @@
             value = value + pltpu.roll(value, shift, 1)
         return value
 
-    out_ref[8:16, :] = fold(jnp.broadcast_to(virt, (8, 128)))
+    virt_ref[...] = fold(jnp.broadcast_to(virt, (8, 128)))[0:1, 0:8]
     for m in range(1, 16):
         z = (cz + 8 - m // 2) % 8
         which = core if m % 2 == 0 else other
         gathered(line, z * 2 + which, l_send.at[m], l_recv.at[m])
     total = jnp.broadcast_to(jnp.sum(line[...], axis=0), (8, 128))
-    out_ref[0:8, :] = fold(jnp.where(lane8 // 8 == sub8, total, 0.0))
+    pair_ref[...] = fold(jnp.where(lane8 // 8 == sub8, total, 0.0))[:, 0:8]
     for copy in pending:
         copy.wait_send()
 
@@ -363,11 +372,11 @@
     eps = jnp.tile(virt_energy.astype(F32), 16).reshape(1, 128)
     vmem = pl.BlockSpec(memory_space=pltpu.VMEM)
     dma = pltpu.SemaphoreType.DMA
-    out = pl.pallas_call(
+    pair, virt = pl.pallas_call(
         kernel,
-        out_shape=jax.ShapeDtypeStruct((16, 128), F32),
+        out_shape=[jax.ShapeDtypeStruct((8, 8), F32), jax.ShapeDtypeStruct((1, 8), F32)],
         in_specs=[pl.BlockSpec(memory_space=pl.ANY), vmem, pl.BlockSpec(memory_space=pltpu.SMEM), vmem],
-        out_specs=vmem,
+        out_specs=[vmem, vmem],
         scratch_shapes=[
             pltpu.VMEM((128, naux // 2), jnp.bfloat16),
             pltpu.VMEM((CHUNKS, NSLOT, 128, width), jnp.bfloat16),
@@ -383,8 +392,8 @@
             pltpu.VMEM((1, 128), F32),
             pltpu.VMEM((16, 1, 128), F32),
             pltpu.VMEM((16, 1, 128), F32),
-            dma(()),
-            dma((3,)), dma((3,)),
+            dma((2,)),
+            dma((4,)), dma((4,)),
             dma((CHUNKS, NSLOT)), dma((CHUNKS, NSLOT)),
             dma((NSLOT,)), dma((NSLOT,)),
             dma((4,)), dma((4,)),
@@ -398,7 +407,7 @@
     )(
         orbital_factors.reshape(-1, naux), eps, occ_energy.astype(F32), jnp.asarray(weight_table()),
     )
-    return out[0:8, 0:8], out[8, 0:8]
+    return pair, virt.reshape(8)
 
 
 def solution(mesh):

time: 99.4 us -> 96.4 us (0.970)
  Pallas kernels: 94.1 us -> 92 us
    pallas_call x1, Pallas kernels: 94.1 us -> 92 us  [on_device(): pl.pallas_call(kernel, out_shape=[jax.ShapeDtypeStruct((8, 8), F32), jax....]
    slice x1 -> x0, local copies, waits for them, and re-layouts: 1.26 us -> none  [on_device(): return (out[0:8, 0:8], out[8, 0:8])]
    squeeze x1 -> x0, local copies, waits for them, and re-layouts: 1.19 us -> none  [on_device(): return (out[0:8, 0:8], out[8, 0:8])]
    unnamed x4 -> x8, local copies, waits for them, and re-layouts: 0.79 us -> 1.84 us
where the time goes in v4:
time: 96.4 us; the launch traced here: 96.2 us
  Pallas kernels  92 us (95%)
  local copies, waits for them, and re-layouts  3.1 us (3%)
    pallas_call x1, Pallas kernels, on_device(): pl.pallas_call(kernel, out_shape=[jax.ShapeDtypeStruct((8, 8), F32), jax....  92 us

profile of v4, /device:TPU:1, one launch (start us, length us, event | category | flops | bytes accessed | tf_op | source)
XLA Modules:
  0.0 96.2 jit_solution(2396449473866646013)
XLA Ops:
  0.6 0.7 tile.2
  1.3 0.0 copy-start.1
  1.3 0.6 reshape_tile.3.eps_ref
  1.9 0.1 copy-done.1
  1.9 0.5 convert_element_type.7.occ_ref
  2.5 92.0 %shard_map.59 = (f32[8,8]{1,0:T(8,128)}, f32[1,8]{1,0:T(1,128)}) custom-call(bf16[64,6144]{1,0:T(8,128)(2,1)} %bitcast.2, f32[1,128]{1,0:T(1,128)} %reshape_tile.3.eps_ref, f32[8]{0:T(128)} %convert_element_type.7.occ_ref, f32[10,1,128]{2,1,0:T(1,128)} %constant.2.clone.weight_ref), custom_call_target="tpu_custom_call" | custom-call | tf_op jit(solution)/shard_map/pallas_call | solution.py:375
  94.4 0.0 copy-start
  94.4 0.7 copy-done
  95.1 0.0 copy-start.2
  95.1 0.6 copy.8
  95.7 0.0 copy-done.2
  95.7 0.5 copy.9
Async XLA Ops:
  1.3 0.7 copy-start.1
  94.4 0.7 copy-start
  95.1 0.6 copy-start.2
